TPU v7x, 32 devices: a whole 2x2x4 slice. The times are simulated.
32 devices in a mesh: data: 2 (over x), dap2: 4 (over z), dap: 4 (over y, core).
Axes of the slice: x: 2, y: 2, z: 4, core: 2. Of those that a mesh axis runs over, the one named last changes fastest.
Arguments:
- pair_act: float32 [1280, 640, 128], P(('data', 'dap'), 'dap2'), parts along dimension 0
- pair_mask: int32 [1280, 640], P(('data', 'dap'), 'dap2'), parts along dimension 0
- ln_z: bfloat16 [1, 2, 2, 128], replicated
- w_ab: bfloat16 [1, 2, 128, 512], replicated
- w_g: bfloat16 [1, 2, 128, 128], replicated
- ln_x: bfloat16 [1, 2, 2, 128], replicated
- w_o: bfloat16 [1, 2, 128, 128], replicated
Outputs:
- output: float32 [1280, 640, 128], P(('data', 'dap'), 'dap2'), parts along dimension 0
There are 2 independent parts. A program takes and returns all parts, laid end to end along the dimension named above; an argument that names none is the same for every part.
All inputs are finite; a program needn't handle non-finite values.
Results may differ from a plain program's by a relative error of at most 0.00132326.
Values are sent between devices in bfloat16 or wider.
A program may use at most 1 GiB of HBM per device.

v0:
```python
import jax
import jax.numpy as jnp
from jax import lax
from jax.sharding import PartitionSpec as P

LN_EPS = 1e-5


def norm_last(values, params):
    mean = jnp.mean(values, axis=-1, keepdims=True)
    centered = values - mean
    variance = jnp.mean(centered * centered, axis=-1, keepdims=True)
    scaled = centered * lax.rsqrt(variance + LN_EPS)
    return (scaled * params[0].astype(jnp.float32) + params[1].astype(jnp.float32)).astype(jnp.bfloat16)


def norm_chan(values, params):
    mean = jnp.mean(values, axis=-3, keepdims=True)
    centered = values - mean
    variance = jnp.mean(centered * centered, axis=-3, keepdims=True)
    scaled = centered * lax.rsqrt(variance + LN_EPS)
    gain = params[0].astype(jnp.float32)[:, None, None]
    bias = params[1].astype(jnp.float32)[:, None, None]
    return (scaled * gain + bias).astype(jnp.bfloat16)


def project_local(z_norm, keep_mask, w_ab):
    hidden = w_ab.shape[1] // 4
    projected = jnp.einsum("ijd,de->eij", z_norm, w_ab, preferred_element_type=jnp.float32)
    a_proj = (keep_mask * jax.nn.sigmoid(projected[hidden:2 * hidden]) * projected[:hidden]).astype(jnp.bfloat16)
    b_proj = (keep_mask * jax.nn.sigmoid(projected[3 * hidden:]) * projected[2 * hidden:3 * hidden]).astype(jnp.bfloat16)
    return a_proj, b_proj


def finish_local(pair_state, z_norm, x_sum, ln_x, w_g, w_o):
    x_norm = norm_chan(x_sum, ln_x)
    update_val = jnp.einsum("cij,cd->ijd", x_norm, w_o, preferred_element_type=jnp.float32)
    gate_val = jax.nn.sigmoid(jnp.einsum("ijd,de->ije", z_norm, w_g, preferred_element_type=jnp.float32))
    return pair_state + gate_val * update_val


def to_transposed(blocks, row_devs, col_devs):
    hidden, n_rows, n_cols = blocks.shape
    n_full = n_rows * row_devs
    fine_rows = n_full // (row_devs * col_devs)
    stage_one = lax.all_to_all(blocks, "dap2", 1, 2, tiled=True)
    stage_one = stage_one.reshape(hidden, fine_rows, row_devs, col_devs * fine_rows)
    stage_two = lax.all_to_all(stage_one, "dap2", 3, 1, tiled=True)
    stage_three = lax.all_to_all(stage_two, "dap", 2, 1, tiled=True)
    stage_three = stage_three.reshape(hidden, n_full, fine_rows)
    return lax.all_to_all(stage_three, "dap2", 1, 2, tiled=True)


def solution(mesh):
    row_devs = mesh.shape["dap"]
    col_devs = mesh.shape["dap2"]
    pair_spec = P(("data", "dap"), "dap2", None)
    mask_spec = P(("data", "dap"), "dap2")

    def tri_update(pair_state, keep_mask, ln_z, w_ab, w_g, ln_x, w_o, outgoing):
        z_norm = norm_last(pair_state, ln_z)
        a_proj, b_proj = project_local(z_norm, keep_mask, w_ab)
        if outgoing:
            a_rows = lax.all_gather(a_proj, "dap2", axis=2, tiled=True)
            b_rows = lax.all_gather(to_transposed(b_proj, row_devs, col_devs), "dap", axis=2, tiled=True)
            x_sum = jnp.einsum("cik,cjk->cij", a_rows, b_rows, preferred_element_type=jnp.float32)
        else:
            a_cols = lax.all_gather(to_transposed(a_proj, row_devs, col_devs), "dap2", axis=1, tiled=True)
            b_cols = lax.all_gather(b_proj, "dap", axis=1, tiled=True)
            x_sum = jnp.einsum("cki,ckj->cij", a_cols, b_cols, preferred_element_type=jnp.float32)
        return finish_local(pair_state, z_norm, x_sum, ln_x, w_g, w_o)

    def local_stack(pair_act, pair_mask, ln_z, w_ab, w_g, ln_x, w_o):
        keep_mask = pair_mask.astype(jnp.float32)
        pair_state = pair_act
        for layer in range(w_o.shape[0]):
            pair_state = tri_update(pair_state, keep_mask, ln_z[layer, 0], w_ab[layer, 0], w_g[layer, 0], ln_x[layer, 0], w_o[layer, 0], True)
            pair_state = tri_update(pair_state, keep_mask, ln_z[layer, 1], w_ab[layer, 1], w_g[layer, 1], ln_x[layer, 1], w_o[layer, 1], False)
        return pair_state

    return jax.shard_map(local_stack, mesh=mesh, in_specs=(pair_spec, mask_spec, P(), P(), P(), P(), P()), out_specs=pair_spec, check_vma=False)
```

profile of v0, /device:TPU:0, one launch (start us, length us, event | category | flops | bytes accessed | tf_op | source)
XLA Modules:
  0.0 2395.9 jit_solution(301202865140912921)
XLA Ops:
  30.1 17.4 convolution_bitcast_fusion.1
  47.5 23.3 fusion.10
  70.9 322.8 %all_to_all.132 = bf16[128,160,160]{0,2,1:T(8,128)(2,1)} all-to-all(bf16[128,160,160]{0,2,1:T(8,128)(2,1)} %get-tuple-element.7), channel_id=1, replica_groups=mesh['data'=2,'dap2'=4,'dap'=4] {'dap2'}, dimensions={1} | all-to-all | bytes 13107200 | tf_op jit(solution)/shard_map/all_to_all | solution.py:46
  404.3 311.9 %all_to_all.133 = bf16[128,40,4,160]{0,2,1,3:T(4,128)(2,1)S(1)} all-to-all(bf16[128,40,4,160]{0,2,1,3:T(4,128)(2,1)} %bitcast.100), channel_id=1, replica_groups=mesh['data'=2,'dap2'=4,'dap'=4] {'dap2'}, dimensions={3} | all-to-all | bytes 13107200 | tf_op jit(solution)/shard_map/all_to_all | solution.py:48
  721.1 76.1 %all_to_all.134 = bf16[128,160,4,40]{0,3,1,2:T(8,128)(2,1)S(1)} all-to-all(bf16[128,160,4,40]{0,3,1,2:T(8,128)(2,1)S(1)} %copy.53), channel_id=1, replica_groups=mesh['data'=2,'dap2'=4,'dap'=4] {'dap'}, dimensions={2} | all-to-all | bytes 13107200 | tf_op jit(solution)/shard_map/all_to_all | solution.py:49
  797.2 146.7 %all_to_all.135 = bf16[128,640,40]{0,2,1:T(8,128)(2,1)S(1)} all-to-all(bf16[128,640,40]{0,2,1:T(8,128)(2,1)S(1)} %bitcast.103), channel_id=1, replica_groups=mesh['data'=2,'dap2'=4,'dap'=4] {'dap2'}, dimensions={1} | all-to-all | bytes 13107200 | tf_op jit(solution)/shard_map/all_to_all | solution.py:51
  951.1 14.4 fusion.36
  965.4 34.2 %copy.56 = bf16[128,160,640]{2,1,0:T(8,128)(2,1)} copy(bf16[128,160,640]{0,2,1:T(8,128)(2,1)} %all-gather.5.cloned.1.call-done) | data formatting | bytes 52428800 | tf_op jit(solution)/shard_map/all_gather | solution.py:64
  999.6 121.4 %all-gather.7.cloned.1.call-done = bf16[128,160,640]{0,1,2:T(8,128)(2,1)} async-done(((bf16[128,160,160]{0,1,2:T(8,128)(2,1)}), bf16[128,160,640]{0,1,2:T(8,128)(2,1)}) %all-gather.7.cloned.1.call-update) | async-done | bytes 26214416 | tf_op jit(solution)/shard_map/all_gather | solution.py:65
  1121.0 37.8 %copy.57 = bf16[128,160,640]{2,1,0:T(8,128)(2,1)} copy(bf16[128,160,640]{0,1,2:T(8,128)(2,1)} %all-gather.7.cloned.1.call-done) | data formatting | bytes 52428800 | tf_op jit(solution)/shard_map/all_gather | solution.py:65
  1158.9 25.6 %fusion.42 = (f32[160,160]{1,0:T(8,128)S(1)}, f32[128,160,160]{2,1,0:T(8,128)}) fusion(bf16[128,160,640]{2,1,0:T(8,128)(2,1)} %copy.56, bf16[128,160,640]{2,1,0:T(8,128)(2,1)} %copy.57), kind=kOutput, calls=%fused_computation.76 | convolution fusion | flops 4197555200 | bytes 65638400 | tf_op jit(solution)/shard_map/cik,cjk->cij/dot_general | solution.py:66
  1204.0 29.0 %fusion.43 = (f32[160,160]{1,0:T(8,128)S(1)}, f32[160,160,128]{2,1,0:T(8,128)}) fusion(f32[160,160,128]{2,1,0:T(8,128)} %param.7, bf16[1,2,128,128]{3,2,1,0:T(8,128)(2,1)S(1)} %copy-done.16, bf16[128,160,160]{2,1,0:T(8,128)(2,1)} %add_convert_fusion.1, f32[160,160,128]{2,1,0:T(8,128)} %fusion.36), kind=kOutput, calls=%fused_computation.77 | convolution fusion | flops 858496000 | bytes 46010368 | tf_op jit(solution)/shard_map/cij,cd->ijd/dot_general | solution.py:37
  1245.1 17.4 convolution_bitcast_fusion
  1262.5 23.4 fusion
  1286.0 151.0 %all_to_all.136 = bf16[128,160,160]{0,2,1:T(8,128)(2,1)} all-to-all(bf16[128,160,160]{0,2,1:T(8,128)(2,1)} %get-tuple-element.6), channel_id=1, replica_groups=mesh['data'=2,'dap2'=4,'dap'=4] {'dap2'}, dimensions={1} | all-to-all | bytes 13107200 | tf_op jit(solution)/shard_map/all_to_all | solution.py:46
  1447.6 147.3 %all_to_all.137 = bf16[128,40,4,160]{0,2,1,3:T(4,128)(2,1)S(1)} all-to-all(bf16[128,40,4,160]{0,2,1,3:T(4,128)(2,1)} %bitcast.107), channel_id=1, replica_groups=mesh['data'=2,'dap2'=4,'dap'=4] {'dap2'}, dimensions={3} | all-to-all | bytes 13107200 | tf_op jit(solution)/shard_map/all_to_all | solution.py:48
  1599.9 76.1 %all_to_all.138 = bf16[128,160,4,40]{0,3,1,2:T(8,128)(2,1)S(1)} all-to-all(bf16[128,160,4,40]{0,3,1,2:T(8,128)(2,1)S(1)} %copy.62), channel_id=1, replica_groups=mesh['data'=2,'dap2'=4,'dap'=4] {'dap'}, dimensions={2} | all-to-all | bytes 13107200 | tf_op jit(solution)/shard_map/all_to_all | solution.py:49
  1675.9 146.6 %all_to_all.139 = bf16[128,640,40]{0,2,1:T(8,128)(2,1)S(1)} all-to-all(bf16[128,640,40]{0,2,1:T(8,128)(2,1)S(1)} %bitcast.110), channel_id=1, replica_groups=mesh['data'=2,'dap2'=4,'dap'=4] {'dap2'}, dimensions={1} | all-to-all | bytes 13107200 | tf_op jit(solution)/shard_map/all_to_all | solution.py:51
  1826.4 14.5 fusion.33
  1840.8 56.7 %copy.65 = bf16[128,640,160]{2,1,0:T(8,128)(2,1)} copy(bf16[128,640,160]{0,2,1:T(8,128)(2,1)} %all-gather.11.cloned.1.call-done) | data formatting | bytes 52428800 | tf_op jit(solution)/shard_map/all_gather | solution.py:69
  1897.5 381.0 %all-gather.9.cloned.1.call-done = bf16[128,640,160]{0,2,1:T(8,128)(2,1)} async-done(((bf16[128,160,160]{0,2,1:T(8,128)(2,1)}), bf16[128,640,160]{0,2,1:T(8,128)(2,1)}) %all-gather.9.cloned.1.call-update) | async-done | bytes 26214416 | tf_op jit(solution)/shard_map/all_gather | solution.py:68
  2278.5 37.8 %copy.64 = bf16[128,640,160]{1,2,0:T(8,128)(2,1)} copy(bf16[128,640,160]{0,2,1:T(8,128)(2,1)} %all-gather.9.cloned.1.call-done) | data formatting | bytes 52428800 | tf_op jit(solution)/shard_map/all_gather | solution.py:68
  2316.3 30.7 %fusion.44 = (f32[160,160]{1,0:T(8,128)S(1)}, f32[128,160,160]{2,1,0:T(8,128)}) fusion(bf16[128,640,160]{1,2,0:T(8,128)(2,1)} %copy.64, bf16[128,640,160]{2,1,0:T(8,128)(2,1)} %copy.65), kind=kOutput, calls=%fused_computation.78 | convolution fusion | flops 4197555200 | bytes 65638400 | tf_op jit(solution)/shard_map/cki,ckj->cij/dot_general | solution.py:70
  2366.6 22.6 multiply_add_fusion
  (75 shorter events, 116.8 us)
Async XLA Ops:
  6.5 958.9 %all-gather.5.cloned.1.call-start = ((), (), s32[]{:S(2)}) async-start(), calls=%async_computation.8 | async-start | bytes 32768000 | tf_op jit(solution)/shard_map/all_gather | solution.py:64
  7.8 22.2 copy-start.8
  7.8 22.2 copy-start.6
  18.1 12.0 copy-start
  30.1 17.4 copy-start.4
  70.8 1050.2 %all-gather.7.cloned.1.call-start = ((), (), s32[]{:S(2)}) async-start(), calls=%async_computation.9 | async-start | bytes 32768000 | tf_op jit(solution)/shard_map/all_gather | solution.py:65
  945.1 5.4 copy-start.13
  945.1 6.0 copy-start.9
  950.5 890.4 %all-gather.11.cloned.1.call-start = ((), (), s32[]{:S(2)}) async-start(), calls=%async_computation.11 | async-start | bytes 32768000 | tf_op jit(solution)/shard_map/all_gather | solution.py:69
  1184.4 13.0 copy-start.2
  1197.5 6.6 copy-start.16
  1233.1 12.0 copy-start.3
  1233.1 12.0 copy-start.7
  1233.1 12.0 copy-start.11
  1233.1 12.0 copy-start.12
  1245.1 17.4 copy-start.5
  1286.0 992.5 %all-gather.9.cloned.1.call-start = ((), (), s32[]{:S(2)}) async-start(), calls=%async_computation.10 | async-start | bytes 32768000 | tf_op jit(solution)/shard_map/all_gather | solution.py:68
  1822.6 3.8 copy-start.10
  2346.9 13.0 copy-start.1
  2346.9 13.0 copy-start.14
  2346.9 13.0 copy-start.15
  2360.0 6.6 copy-start.17
Sparse Core Ops, SparseCore 0:
  70.9 714.1 all-gather.4
  950.6 170.4 all-gather.6
  1286.1 161.4 all-gather.10
  1826.5 451.9 all-gather.8
where the time goes:
time: 2410 us; the launch traced here: 2400 us
  blocking collectives  1380 us (57%)
  waiting for transfers between devices  503 us (21%)
  local copies, waits for them, and re-layouts  215 us (9%)
  matrix products  172 us (7%)
  other arithmetic  115 us (5%)
    all_to_all x2, blocking collectives, to_transposed(): stage_one = lax.all_to_all(blocks, 'dap2', 1, 2, tiled=True)  474 us
    all_to_all x2, blocking collectives, to_transposed(): stage_two = lax.all_to_all(stage_one, 'dap2', 3, 1, tiled=True)  459 us
    all_gather x1, waiting for transfers between devices, tri_update(): lax.all_gather(to_transposed(a_proj, row_devs, col_devs), 'dap2', axis=1,...  381 us
    all_to_all x2, blocking collectives, to_transposed(): return lax.all_to_all(stage_three, 'dap2', 1, 2, tiled=True)  293 us
    all_to_all x2, blocking collectives, to_transposed(): stage_three = lax.all_to_all(stage_two, 'dap', 2, 1, tiled=True)  152 us
    all_gather x1, waiting for transfers between devices, tri_update(): lax.all_gather(to_transposed(b_proj, row_devs, col_devs), 'dap', axis=2,...  121 us
    all_gather x1, local copies, waits for them, and re-layouts, tri_update(): b_cols = lax.all_gather(b_proj, 'dap', axis=1, tiled=True)  56.7 us
    dot_general x2, matrix products, finish_local(): jnp.einsum('cij,cd->ijd', x_norm, w_o, preferred_element_type=jnp.float32)  51.6 us
  transfers between devices with their start and end apart: 4, of which 2 were waited for; matrix products, arithmetic and copies ran while one was open for 7% of the time, Pallas kernels for 0%

commit v1 on v0

v1 whole, which is shorter than its diff:
```python
import functools

import jax
import jax.numpy as jnp
from jax import lax
from jax.experimental import pallas as pl
from jax.experimental.pallas import tpu as pltpu
from jax.sharding import PartitionSpec as P

LN_EPS = 1e-5
GROUP = 16
CHAN_BLOCK = 16
CHUNKS = 8
F32 = jnp.float32
BF16 = jnp.bfloat16
MESH = pl.DeviceIdType.MESH


def sigmoid(v):
    return 0.5 * jnp.tanh(0.5 * v) + 0.5


def layer_norm_rows(v, params):
    mean = jnp.mean(v, axis=-1, keepdims=True)
    centered = v - mean
    variance = jnp.mean(centered * centered, axis=-1, keepdims=True)
    return centered * lax.rsqrt(variance + LN_EPS) * params[0:1, :] + params[1:2, :]


def norm_kernel(slot_ref, z_ref, mask_ref, ln_ref, out_ref):
    ln = ln_ref[...]
    mask = mask_ref[0]
    for ii in range(GROUP):
        zn = layer_norm_rows(z_ref[ii], ln) * mask[:, ii:ii + 1]
        out_ref[0, ii] = zn.astype(BF16)


def first_norm(z, mask_g, ln, slot, n_slots):
    rows, cols, width = z.shape
    return pl.pallas_call(
        norm_kernel,
        out_shape=jax.ShapeDtypeStruct((n_slots, rows, cols, width), BF16),
        grid_spec=pltpu.PrefetchScalarGridSpec(
            num_scalar_prefetch=1,
            grid=(rows // GROUP,),
            in_specs=[
                pl.BlockSpec((GROUP, cols, width), lambda g, s: (g, 0, 0)),
                pl.BlockSpec((1, cols, GROUP), lambda g, s: (g, 0, 0)),
                pl.BlockSpec((2, width), lambda g, s: (0, 0)),
            ],
            out_specs=pl.BlockSpec((1, GROUP, cols, width), lambda g, s: (s[0], g, 0, 0)),
        ),
        name="first_norm",
    )(slot, z, mask_g, ln)


def chunk_of(ref, slot, h, step):
    return ref.at[slot, pl.ds(h * step, step)]


def greet(z, r, n_z):
    barrier = pltpu.get_barrier_semaphore()

    def hello(where):
        pl.semaphore_signal(barrier, inc=1, device_id=where, device_id_type=MESH)

    for m in (1, 2, 3):
        hello({"dap": r ^ m})
    pl.when(z > 0)(lambda: hello({"dap2": z - 1}))
    pl.when(z < n_z - 1)(lambda: hello({"dap2": z + 1}))
    inner = (z > 0) & (z < n_z - 1)
    pl.when(inner)(lambda: pl.semaphore_wait(barrier, 5))
    pl.when(jnp.logical_not(inner))(lambda: pl.semaphore_wait(barrier, 4))


def copy_to(buf, src, dst, h, step, send_sem, recv_sem, where):
    return pltpu.make_async_remote_copy(
        src_ref=chunk_of(buf, src, h, step),
        dst_ref=chunk_of(buf, dst, h, step),
        send_sem=send_sem,
        recv_sem=recv_sem,
        device_id=where,
        device_id_type=MESH,
    )


def line_copies(buf, z, step, n_z, send_r, send_l, recv_z):
    def right(slot, h):
        return copy_to(buf, slot, slot, h, step, send_r.at[slot, h], recv_z.at[slot, h], {"dap2": z + 1})

    def left(slot, h):
        return copy_to(buf, slot, slot, h, step, send_l.at[slot, h], recv_z.at[slot, h], {"dap2": z - 1})

    return right, left


def start_line(right, left, z, n_z):
    @pl.loop(0, CHUNKS)
    def _(h):
        pl.when(z < n_z - 1)(lambda: right(z, h).start())
        pl.when(z > 0)(lambda: left(z, h).start())


def arrive_line(right, left, z, t, h, n_z, on_arrival):
    @pl.when(z - t >= 0)
    def _():
        right(z - t, h).wait_recv()
        pl.when(z < n_z - 1)(lambda: right(z - t, h).start())
        on_arrival(z - t, h)

    @pl.when(z + t < n_z)
    def _():
        left(z + t, h).wait_recv()
        pl.when(z > 0)(lambda: left(z + t, h).start())
        on_arrival(z + t, h)


def drain_line(right, left, z, n_z):
    for t in range(n_z):
        @pl.loop(0, CHUNKS)
        def _(h):
            pl.when((z - t >= 0) & (z < n_z - 1))(lambda: right(z - t, h).wait_send())
            pl.when((z + t < n_z) & (z > 0))(lambda: left(z + t, h).wait_send())


def relay_out_kernel(n_z, src_ref, buf, send_r, send_l, recv_z, send_p, send_q, recv_b, send_f):
    z = lax.axis_index("dap2")
    r = lax.axis_index("dap")
    step = buf.shape[1] // CHUNKS
    greet(z, r, n_z)
    right, left = line_copies(buf, z, step, n_z, send_r, send_l, recv_z)

    def to_near(slot, h):
        return copy_to(buf, slot, n_z + slot, h, step, send_p.at[slot, h], recv_b.at[slot, h], {"dap": r ^ 1})

    def to_far(slot, h):
        return copy_to(buf, slot, n_z + slot, h, step, send_q.at[slot, h], recv_b.at[slot, h], {"dap": r ^ 2})

    def onward(slot, h):
        return copy_to(buf, n_z + slot, n_z + slot, h, step, send_f.at[slot, h], recv_b.at[slot, h], {"dap": r ^ 1})

    def spread(slot, h):
        @pl.when(r == z)
        def _():
            to_far(slot, h).start()
            to_near(slot, h).start()

    def pass_on(slot, h):
        @pl.when(r == z ^ 2)
        def _():
            onward(slot, h).wait_recv()
            onward(slot, h).start()

    def pass_on_step(t, h):
        pl.when(z - t >= 0)(lambda: pass_on(z - t, h))
        pl.when(z + t < n_z)(lambda: pass_on(z + t, h))

    start_line(right, left, z, n_z)
    pl.loop(0, CHUNKS)(lambda h: spread(z, h))
    for t in range(1, n_z):
        @pl.loop(0, CHUNKS)
        def _(h):
            arrive_line(right, left, z, t, h, n_z, spread)
            if t == 1:
                pass_on(z, h)

                @pl.when(h >= 2)
                def _():
                    pass_on_step(1, h - 2)
            else:
                @pl.when(h >= 2)
                def _():
                    pass_on_step(t, h - 2)

                @pl.when(h < 2)
                def _():
                    pass_on_step(t - 1, h + CHUNKS - 2)
    for h in (CHUNKS - 2, CHUNKS - 1):
        pass_on_step(n_z - 1, h)
    drain_line(right, left, z, n_z)
    for slot in range(n_z):
        @pl.loop(0, CHUNKS)
        def _(h):
            @pl.when(r == z)
            def _():
                to_far(slot, h).wait_send()
                to_near(slot, h).wait_send()

            @pl.when(r == z ^ 2)
            def _():
                onward(slot, h).wait_send()

            @pl.when((r == z ^ 1) | (r == z ^ 3))
            def _():
                onward(slot, h).wait_recv()


def relay_in_kernel(n_z, src_ref, buf, send_r, send_l, recv_z, send_a, recv_a, send_p, send_q, recv_b, send_f):
    z = lax.axis_index("dap2")
    r = lax.axis_index("dap")
    step = buf.shape[1] // CHUNKS
    greet(z, r, n_z)
    right, left = line_copies(buf, z, step, n_z, send_r, send_l, recv_z)

    def to_owner(slot, h):
        return copy_to(buf, slot, n_z + r, h, step, send_a.at[slot, h], recv_a.at[r, h], {"dap": slot})

    def from_peer(peer, h):
        return copy_to(buf, r, n_z + peer, h, step, send_a.at[peer, h], recv_a.at[peer, h], {"dap": peer})

    def to_near(h):
        return copy_to(buf, z, 2 * n_z + r, h, step, send_p.at[h], recv_b.at[r, h], {"dap": r ^ 1})

    def to_far(h):
        return copy_to(buf, z, 2 * n_z + r, h, step, send_q.at[h], recv_b.at[r, h], {"dap": r ^ 2})

    def onward(h):
        return copy_to(buf, 2 * n_z + (r ^ 2), 2 * n_z + (r ^ 2), h, step, send_f.at[h], recv_b.at[r ^ 2, h], {"dap": r ^ 1})

    def from_b(peer, h):
        return copy_to(buf, z, 2 * n_z + peer, h, step, send_p.at[h], recv_b.at[peer, h], {"dap": r ^ 1})

    def spread(slot, h):
        @pl.when(slot != r)
        def _():
            to_owner(slot, h).start()

    start_line(right, left, z, n_z)

    @pl.loop(0, CHUNKS)
    def _(h):
        to_far(h).start()
        to_near(h).start()

    for t in range(1, n_z):
        @pl.loop(0, CHUNKS)
        def _(h):
            arrive_line(right, left, z, t, h, n_z, spread)
            if t == 2:
                onward(h).wait_recv()
                onward(h).start()

    drain_line(right, left, z, n_z)

    @pl.loop(0, CHUNKS)
    def _(h):
        to_far(h).wait_send()
        to_near(h).wait_send()
        onward(h).wait_send()
        from_b(r ^ 1, h).wait_recv()
        from_b(r ^ 3, h).wait_recv()
        for slot in range(n_z):
            @pl.when((slot != z) & (slot != r))
            def _():
                to_owner(slot, h).wait_send()
        for m in (1, 2, 3):
            @pl.when(r != z)
            def _():
                from_peer(r ^ m, h).wait_recv()


def relay(kernel, buf, sems, collective_id, name):
    return pl.pallas_call(
        kernel,
        out_shape=jax.ShapeDtypeStruct(buf.shape, buf.dtype),
        in_specs=[pl.BlockSpec(memory_space=pl.ANY)],
        out_specs=pl.BlockSpec(memory_space=pl.ANY),
        scratch_shapes=[pltpu.SemaphoreType.DMA(s) for s in sems],
        input_output_aliases={0: 0},
        compiler_params=pltpu.CompilerParams(collective_id=collective_id, has_side_effects=True),
        name=name,
    )(buf)


def project_kernel(slots_ref, x0, x1, x2, x3, w_ref, out_ref, stage):
    hidden = out_ref.shape[1]
    parts = out_ref.shape[3] // 128
    w_t = w_ref[0]

    def one_row(ii, carry):
        zn = jnp.concatenate([x[0, ii] for x in (x0, x1, x2, x3)], axis=0)
        q = lax.dot_general(w_t, zn, (((1,), (1,)), ((), ())), preferred_element_type=F32)
        val = sigmoid(q[hidden:]) * q[:hidden]
        for p in range(parts):
            stage[p, pl.ds(ii, hidden, stride=GROUP), :] = val[:, p * 128:(p + 1) * 128]
        return carry

    lax.fori_loop(0, GROUP, one_row, 0, unroll=2)
    for p in range(parts):
        out_ref[0, :, :, p * 128:(p + 1) * 128] = stage[p].reshape(hidden, GROUP, 128).astype(BF16)


def project(buf, slots, w_abt):
    _, rows, cols, width = buf.shape
    hidden = w_abt.shape[1] // 2
    depth = 4 * cols

    def block(k):
        return pl.BlockSpec((1, GROUP, cols, width), lambda o, g, s: (s[4 * o + k], g, 0, 0))

    return pl.pallas_call(
        project_kernel,
        out_shape=jax.ShapeDtypeStruct((2, hidden, rows, depth), BF16),
        grid_spec=pltpu.PrefetchScalarGridSpec(
            num_scalar_prefetch=1,
            grid=(2, rows // GROUP),
            in_specs=[block(0), block(1), block(2), block(3), pl.BlockSpec((1, 2 * hidden, width), lambda o, g, s: (o, 0, 0))],
            out_specs=pl.BlockSpec((1, hidden, GROUP, depth), lambda o, g, s: (o, 0, g, 0)),
            scratch_shapes=[pltpu.VMEM((depth // 128, hidden * GROUP, 128), F32)],
        ),
        name="project",
    )(slots, buf, buf, buf, buf, w_abt)


def finish_kernel(n_mul, emit, slot_ref, a_ref, b_ref, z_ref, lnz_ref, wg_ref, lnx_ref, wo_ref, *rest):
    if emit:
        mask_ref, ln2_ref, out_ref, next_ref, x_lo, x_hi, turn = rest
    else:
        out_ref, x_lo, x_hi = rest
    rows = a_ref.shape[2]
    cols = z_ref.shape[1]
    hidden = wo_ref.shape[0]
    lo = min(cols, 128)
    s = pl.program_id(0)

    @pl.when(s < n_mul)
    def _():
        for cc in range(CHAN_BLOCK):
            x = lax.dot_general(a_ref[0, cc], b_ref[0, cc], (((1,), (1,)), ((), ())), preferred_element_type=F32)
            at = pl.multiple_of((s * CHAN_BLOCK + cc) * rows, 8)
            x_lo[pl.ds(at, rows), :lo] = x[:, :lo]
            if cols > lo:
                x_hi[pl.ds(at, rows), :cols - lo] = x[:, lo:]

    @pl.when(s >= n_mul)
    def _():
        first = (s - n_mul) * GROUP
        ln = lnz_ref[...]
        w_g = wg_ref[...]
        w_o = wo_ref[...]
        gain = lnx_ref[:, 0:1]
        bias = lnx_ref[:, 1:2]
        for ii in range(GROUP):
            x = x_lo[pl.ds(first + ii, hidden, stride=rows), :][:, :lo]
            if cols > lo:
                x = jnp.concatenate([x, x_hi[pl.ds(first + ii, hidden, stride=rows), :][:, :cols - lo]], axis=1)
            mean = jnp.mean(x, axis=0, keepdims=True)
            centered = x - mean
            variance = jnp.mean(centered * centered, axis=0, keepdims=True)
            xn = (centered * lax.rsqrt(variance + LN_EPS) * gain + bias).astype(BF16)
            y = lax.dot_general(xn, w_o, (((0,), (0,)), ((), ())), preferred_element_type=F32)
            z = z_ref[ii]
            zn = layer_norm_rows(z, ln).astype(BF16)
            gate = sigmoid(jnp.dot(zn, w_g, preferred_element_type=F32))
            new = z + gate * y
            out_ref[ii] = new
            if emit:
                zn2 = layer_norm_rows(new, ln2_ref[...]) * mask_ref[0][:, ii:ii + 1]
                turn[pl.ds(ii, cols, stride=GROUP), :] = zn2
        if emit:
            next_ref[0] = turn[...].reshape(cols, GROUP, turn.shape[1]).astype(BF16)


def finish(ab, z, ln_z, w_g, ln_x, w_o, slot, extra=None, n_slots=0):
    rows, cols, width = z.shape
    hidden, depth = ab.shape[1], ab.shape[3]
    n_mul = hidden // CHAN_BLOCK
    groups = rows // GROUP

    def tile(i, sl):
        return (jnp.maximum(i - n_mul, 0), 0, 0)

    def whole(i, sl):
        return (0, 0)

    in_specs = [
        pl.BlockSpec((1, CHAN_BLOCK, rows, depth), lambda i, sl: (0, jnp.minimum(i, n_mul - 1), 0, 0)),
        pl.BlockSpec((1, CHAN_BLOCK, rows, depth), lambda i, sl: (1, jnp.minimum(i, n_mul - 1), 0, 0)),
        pl.BlockSpec((GROUP, cols, width), tile),
        pl.BlockSpec((2, width), whole),
        pl.BlockSpec((width, width), whole),
        pl.BlockSpec((hidden, 2), whole),
        pl.BlockSpec((hidden, width), whole),
    ]
    args = [ab, ab, z, ln_z, w_g, ln_x, w_o]
    out_shape = [jax.ShapeDtypeStruct(z.shape, F32)]
    out_specs = [pl.BlockSpec((GROUP, cols, width), tile)]
    scratch = [pltpu.VMEM((hidden * rows, 128), F32), pltpu.VMEM((hidden * rows, 128), F32)]
    if extra is not None:
        in_specs += [pl.BlockSpec((1, cols, GROUP), tile), pl.BlockSpec((2, width), whole)]
        args += list(extra)
        out_shape.append(jax.ShapeDtypeStruct((n_slots, cols, rows, width), BF16))
        out_specs.append(pl.BlockSpec((1, cols, GROUP, width), lambda i, sl: (sl[0], 0, jnp.maximum(i - n_mul, 0), 0)))
        scratch.append(pltpu.VMEM((cols * GROUP, width), F32))
    return pl.pallas_call(
        functools.partial(finish_kernel, n_mul, extra is not None),
        out_shape=out_shape,
        grid_spec=pltpu.PrefetchScalarGridSpec(
            num_scalar_prefetch=1, grid=(n_mul + groups,), in_specs=in_specs, out_specs=out_specs, scratch_shapes=scratch
        ),
        compiler_params=pltpu.CompilerParams(vmem_limit_bytes=62 * 1024 * 1024),
        name="finish",
    )(slot, *args)


def solution(mesh):
    n_z = mesh.shape["dap2"]
    n_r = mesh.shape["dap"]
    pair_spec = P(("data", "dap"), "dap2", None)
    mask_spec = P(("data", "dap"), "dap2")
    out_sems = [(n_z, CHUNKS)] * 7
    in_sems = [(n_z, CHUNKS)] * 5 + [(CHUNKS,)] * 2 + [(n_r, CHUNKS), (CHUNKS,)]

    def local_stack(pair_act, pair_mask, ln_z, w_ab, w_g, ln_x, w_o):
        z_at = lax.axis_index("dap2").astype(jnp.int32)
        r_at = lax.axis_index("dap").astype(jnp.int32)
        slot = z_at.reshape(1)
        rows, cols, _ = pair_act.shape
        mask_g = pair_mask.astype(F32).T.reshape(cols, rows // GROUP, GROUP).transpose(1, 0, 2)
        k = jnp.arange(n_z, dtype=jnp.int32)
        diag = r_at == z_at
        slots_out = jnp.concatenate([k, jnp.where(diag, k, n_z + k)])
        b_in = jnp.where(k == r_at, z_at, 2 * n_z + k)
        a_in = jnp.where(diag, b_in, jnp.where(k == r_at, r_at, n_z + k))
        slots_in = jnp.concatenate([a_in, b_in])

        state = pair_act
        layers = w_o.shape[0]
        buf = None
        for layer in range(layers):
            for upd in range(2):
                lnz = ln_z[layer, upd].astype(F32)
                w_abt = w_ab[layer, upd].T.reshape(2, -1, w_ab.shape[2])
                lnx = ln_x[layer, upd].astype(F32).T
                if buf is None:
                    buf = first_norm(state, mask_g, lnz, slot, 2 * n_z)
                if upd == 0:
                    buf = relay(functools.partial(relay_out_kernel, n_z), buf, out_sems, 2 * layer, f"relay_out_{layer}")
                    ab = project(buf, slots_out, w_abt)
                    nxt = (mask_g, ln_z[layer, 1].astype(F32))
                    state, buf = finish(ab, state, lnz, w_g[layer, 0], lnx, w_o[layer, 0], slot, nxt, 3 * n_z)
                else:
                    buf = relay(functools.partial(relay_in_kernel, n_z), buf, in_sems, 2 * layer + 1, f"relay_in_{layer}")
                    ab = project(buf, slots_in, w_abt)
                    (state,) = finish(ab, state, lnz, w_g[layer, 1], lnx, w_o[layer, 1], slot)
                    buf = None
        return state

    return jax.shard_map(local_stack, mesh=mesh, in_specs=(pair_spec, mask_spec, P(), P(), P(), P(), P()), out_specs=pair_spec, check_vma=False)
```

time: 2410 us -> 1280 us (0.53)
  blocking collectives: 1380 us -> 0 us
  Pallas kernels: 0 us -> 1270 us
  waiting for transfers between devices: 503 us -> 0 us
  local copies, waits for them, and re-layouts: 215 us -> 4.82 us
  matrix products: 172 us -> 0 us
  other arithmetic: 115 us -> 4.64 us
    all_to_all x8 -> x0, blocking collectives: 1380 us -> none  [the longest x2 474 us: to_transposed(): stage_one = lax.all_to_all(blocks, 'dap2', 1, 2, tiled=True)]
    pallas_call x0 -> x7, Pallas kernels: none -> 1270 us  [the longest x2 875 us: relay(): pl.pallas_call(kernel, out_shape=jax.ShapeDtypeStruct(buf.shape, buf.dtyp...]
    all_gather x4 -> x0, waiting for transfers between devices: 502 us -> none  [the longest x1 381 us: tri_update(): lax.all_gather(to_transposed(a_proj, row_devs, col_devs), 'dap2', axis=1,...]
    dot_general x8 -> x0, matrix products: 172 us -> none  [the longest x2 51.6 us: finish_local(): jnp.einsum('cij,cd->ijd', x_norm, w_o, preferred_element_type=jnp.float32)]
    all_gather x4 -> x0, local copies, waits for them, and re-layouts: 166 us -> none  [the longest x1 56.7 us: tri_update(): b_cols = lax.all_gather(b_proj, 'dap', axis=1, tiled=True)]
    convert_element_type x7 -> x2, other arithmetic: 61.7 us -> 2.14 us  [the longest x1 1.21 us: local_stack(): nxt = (mask_g, ln_z[layer, 1].astype(F32))]
    reduce_sum x5 -> x0, other arithmetic: 53.3 us -> none  [the longest x2 23.8 us: norm_last(): variance = jnp.mean(centered * centered, axis=-1, keepdims=True)]
    all_to_all x11 -> x0, local copies, waits for them, and re-layouts: 41.4 us -> none  [the longest x2 21.3 us: to_transposed(): stage_one = lax.all_to_all(blocks, 'dap2', 1, 2, tiled=True)]
  transfers between devices with their start and end apart: 4 -> 0, of which waited for: 2 -> 0; matrix products, arithmetic and copies ran while one was open for 7% -> 0% of each run, Pallas kernels for 0% -> 0%
where the time goes in v1:
time: 1280 us
  Pallas kernels  1270 us (99%)
    pallas_call x2, Pallas kernels, relay(): pl.pallas_call(kernel, out_shape=jax.ShapeDtypeStruct(buf.shape, buf.dtyp...  875 us
    pallas_call x2, Pallas kernels, project(): pl.pallas_call(project_kernel, out_shape=jax.ShapeDtypeStruct((2, hidden,...  216 us
    pallas_call x2, Pallas kernels, finish(): pl.pallas_call(functools.partial(finish_kernel, n_mul, extra is not None)...  155 us
    pallas_call x1, Pallas kernels, first_norm(): pl.pallas_call(norm_kernel, out_shape=jax.ShapeDtypeStruct((n_slots, rows...  27.7 us

profile of v1, /device:TPU:0, one launch (start us, length us, event | category | flops | bytes accessed | tf_op | source)
XLA Modules:
  0.0 1284.2 jit_solution(16608625261943128929)
XLA Ops:
  0.0 0.6 pad_add_fusion.slots_ref
  0.7 0.6 pad_add_fusion.1.slots_ref
  1.3 0.9 convert_element_type.22
  2.2 1.2 copy.14
  3.4 1.2 bitcast_convert_fusion
  4.6 27.7 %first_norm.1.src_ref = bf16[8,160,160,128]{3,2,1,0:T(8,128)(2,1)} custom-call(s32[1]{0:T(128)} %bitcast.slot_ref, f32[160,160,128]{2,1,0:T(8,128)} %z_ref.3, f32[10,160,16]{2,1,0:T(8,128)} %bitcast.39, f32[2,128]{1,0:T(2,128)} %get-tuple-element.18.ln_ref.lnz_ref), custom_call_target="tpu_custom_call" | custom-call | tf_op jit(solution)/shard_map/first_norm/pallas_call | solution.py:40
  32.3 438.8 %relay_out_0.1.x0.x1.x2.x3 = bf16[8,160,160,128]{3,2,1,0:T(8,128)(2,1)} custom-call(bf16[8,160,160,128]{3,2,1,0:T(8,128)(2,1)} %first_norm.1.src_ref), custom_call_target="tpu_custom_call", output_to_operand_aliasing={{}: (0, {})} | custom-call | tf_op jit(solution)/shard_map/relay_out_0/pallas_call | solution.py:263
  471.1 0.0 copy-done.1
  471.1 0.7 slice_bitcast_fusion
  471.8 0.7 copy.15
  472.5 108.0 %project.2.a_ref.b_ref = bf16[2,128,160,640]{3,2,1,0:T(8,128)(2,1)} custom-call(s32[8]{0:T(128)} %pad_add_fusion.1.slots_ref, bf16[8,160,160,128]{3,2,1,0:T(8,128)(2,1)} %relay_out_0.1.x0.x1.x2.x3, bf16[8,160,160,128]{3,2,1,0:T(8,128)(2,1)} %relay_out_0.1.x0.x1.x2.x3, bf16[8,160,160,128]{3,2,1,0:T(8,128)(2,1)} %relay_out_0.1.x0.x1.x2.x3, ...), custom_call_target="tpu_custom_call" | custom-call | tf_op jit(solution)/shard_map/project/pallas_call | solution.py:301
  580.5 0.0 copy-done.2
  580.6 0.7 slice_bitcast_fusion.2
  581.2 0.5 fusion
  581.7 0.1 copy.16
  581.9 0.6 convert_bitcast_fusion.1.lnx_ref
  582.5 101.8 %finish.2 = (f32[160,160,128]{2,1,0:T(8,128)}, bf16[12,160,160,128]{3,2,1,0:T(8,128)(2,1)}) custom-call(s32[1]{0:T(128)} %bitcast.slot_ref, bf16[2,128,160,640]{3,2,1,0:T(8,128)(2,1)} %project.2.a_ref.b_ref, bf16[2,128,160,640]{3,2,1,0:T(8,128)(2,1)} %project.2.a_ref.b_ref, f32[160,160,128]{2,1,0:T(8,128)} %z_ref.3, ...), custom_call_target="tpu_custom_call" | custom-call | tf_op jit(solution)/shard_map/finish/pallas_call | solution.py:395
  684.3 436.7 %relay_in_0.1.x0.x1.x2.x3 = bf16[12,160,160,128]{3,2,1,0:T(8,128)(2,1)} custom-call(bf16[12,160,160,128]{3,2,1,0:T(8,128)(2,1)} %get-tuple-element.7.src_ref), custom_call_target="tpu_custom_call", output_to_operand_aliasing={{}: (0, {})} | custom-call | tf_op jit(solution)/shard_map/relay_in_0/pallas_call | solution.py:263
  1121.0 0.8 copy.17
  1121.8 108.0 %project.3.a_ref.b_ref = bf16[2,128,160,640]{3,2,1,0:T(8,128)(2,1)} custom-call(s32[8]{0:T(128)} %pad_add_fusion.slots_ref, bf16[12,160,160,128]{3,2,1,0:T(8,128)(2,1)} %relay_in_0.1.x0.x1.x2.x3, bf16[12,160,160,128]{3,2,1,0:T(8,128)(2,1)} %relay_in_0.1.x0.x1.x2.x3, bf16[12,160,160,128]{3,2,1,0:T(8,128)(2,1)} %relay_in_0.1.x0.x1.x2.x3, ...), custom_call_target="tpu_custom_call" | custom-call | tf_op jit(solution)/shard_map/project/pallas_call | solution.py:301
  1229.8 0.0 copy-done.4
  1229.8 0.1 copy.18
  1230.0 0.6 convert_bitcast_fusion.lnx_ref
  1230.6 53.6 %finish.3 = f32[160,160,128]{2,1,0:T(8,128)} custom-call(s32[1]{0:T(128)} %bitcast.slot_ref, bf16[2,128,160,640]{3,2,1,0:T(8,128)(2,1)} %project.3.a_ref.b_ref, bf16[2,128,160,640]{3,2,1,0:T(8,128)(2,1)} %project.3.a_ref.b_ref, f32[160,160,128]{2,1,0:T(8,128)} %get-tuple-element.8.z_ref, f32[2,128]{1,0:T(2,128)} %get-tuple-element.17.rest_1_.lnz_ref, ...), custom_call_target="tpu_custom_call" | custom-call | tf_op jit(solution)/shard_map/finish/pallas_call | solution.py:395
  (12 shorter events, 0.0 us)
Async XLA Ops:
  32.3 438.8 %copy-start.1 = (bf16[1,2,128,512]{3,2,1,0:T(8,128)(2,1)S(1)}, bf16[1,2,128,512]{3,2,1,0:T(8,128)(2,1)}, u32[]{:S(2)}) copy-start(bf16[1,2,128,512]{3,2,1,0:T(8,128)(2,1)} %param.10) | copy-start | bytes 786436
  472.5 108.0 %copy-start.2 = (bf16[1,2,128,128]{3,2,1,0:T(8,128)(2,1)S(1)}, bf16[1,2,128,128]{3,2,1,0:T(8,128)(2,1)}, u32[]{:S(2)}) copy-start(bf16[1,2,128,128]{3,2,1,0:T(8,128)(2,1)} %param.13) | copy-start | bytes 196612
  472.5 108.0 %copy-start.3 = (bf16[1,2,128,128]{3,2,1,0:T(8,128)(2,1)S(1)}, bf16[1,2,128,128]{3,2,1,0:T(8,128)(2,1)}, u32[]{:S(2)}) copy-start(bf16[1,2,128,128]{3,2,1,0:T(8,128)(2,1)} %param.11) | copy-start | bytes 196612
  472.5 108.7 %copy-start.5 = (bf16[1,2,2,128]{3,2,1,0:T(2,128)(2,1)S(1)}, bf16[1,2,2,128]{3,2,1,0:T(2,128)(2,1)}, u32[]{:S(2)}) copy-start(bf16[1,2,2,128]{3,2,1,0:T(2,128)(2,1)} %param.12) | copy-start | bytes 3076
  684.3 436.7 %copy-start = (bf16[512,128]{0,1:T(8,128)(2,1)S(1)}, bf16[512,128]{0,1:T(8,128)(2,1)}, u32[]{:S(2)}) copy-start(bf16[512,128]{0,1:T(8,128)(2,1)} %get-tuple-element.9) | copy-start | bytes 393220
  1121.8 108.0 %copy-start.4 = (bf16[1,1,2,128]{3,2,1,0:T(2,128)(2,1)S(1)}, bf16[1,1,2,128]{3,2,1,0:T(2,128)(2,1)}, u32[]{:S(2)}) copy-start(bf16[1,1,2,128]{3,2,1,0:T(2,128)(2,1)} %get-tuple-element.15) | copy-start | bytes 1540

commit v2 on v0

v2 whole, which is shorter than its diff:
```python
import functools

import jax
import jax.numpy as jnp
from jax import lax
from jax.experimental import pallas as pl
from jax.experimental.pallas import tpu as pltpu
from jax.sharding import PartitionSpec as P

LN_EPS = 1e-5
GROUP = 16
CHAN_BLOCK = 16
PITCH = 24
PAD = 8
LAG_B = 3
LAG_A = 2
F32 = jnp.float32
BF16 = jnp.bfloat16
MESH = pl.DeviceIdType.MESH


def sigmoid(v):
    return 0.5 * jnp.tanh(0.5 * v) + 0.5


def layer_norm_rows(v, params):
    mean = jnp.mean(v, axis=-1, keepdims=True)
    centered = v - mean
    variance = jnp.mean(centered * centered, axis=-1, keepdims=True)
    return centered * lax.rsqrt(variance + LN_EPS) * params[0:1, :] + params[1:2, :]


def greet(z, r, n_z):
    barrier = pltpu.get_barrier_semaphore()

    def hello(where):
        pl.semaphore_signal(barrier, inc=1, device_id=where, device_id_type=MESH)

    for m in (1, 2, 3):
        hello({"dap": r ^ m})
    pl.when(z > 0)(lambda: hello({"dap2": z - 1}))
    pl.when(z < n_z - 1)(lambda: hello({"dap2": z + 1}))
    inner = (z > 0) & (z < n_z - 1)
    pl.when(inner)(lambda: pl.semaphore_wait(barrier, 5))
    pl.when(jnp.logical_not(inner))(lambda: pl.semaphore_wait(barrier, 4))


def copy_to(buf, src, dst, h, send_sem, recv_sem, where):
    rows = pl.ds(h * GROUP, GROUP)
    return pltpu.make_async_remote_copy(
        src_ref=buf.at[src, rows],
        dst_ref=buf.at[dst, rows],
        send_sem=send_sem,
        recv_sem=recv_sem,
        device_id=where,
        device_id_type=MESH,
    )


def line_copies(buf, z, send_r, send_l, recv_z):
    def right(slot, h):
        return copy_to(buf, slot, slot, h, send_r.at[slot, h], recv_z.at[slot, h], {"dap2": z + 1})

    def left(slot, h):
        return copy_to(buf, slot, slot, h, send_l.at[slot, h], recv_z.at[slot, h], {"dap2": z - 1})

    return right, left


def start_line(right, left, z, h, n_z):
    pl.when(z < n_z - 1)(lambda: right(z, h).start())
    pl.when(z > 0)(lambda: left(z, h).start())


def arrive_line(right, left, z, t, h, n_z, on_arrival):
    @pl.when(z - t >= 0)
    def _():
        right(z - t, h).wait_recv()
        pl.when(z < n_z - 1)(lambda: right(z - t, h).start())
        on_arrival(z - t, h)

    @pl.when(z + t < n_z)
    def _():
        left(z + t, h).wait_recv()
        pl.when(z > 0)(lambda: left(z + t, h).start())
        on_arrival(z + t, h)


def drain_line(right, left, z, n_z, chunks):
    for t in range(n_z):
        @pl.loop(0, chunks)
        def _(h):
            pl.when((z - t >= 0) & (z < n_z - 1))(lambda: right(z - t, h).wait_send())
            pl.when((z + t < n_z) & (z > 0))(lambda: left(z + t, h).wait_send())


class Projector:
    def __init__(self, buf, w_ref, ab, x_in, staged, stage, in_sem, out_sem, sources):
        self.refs = buf, w_ref, ab, x_in, staged, stage
        self.sems = in_sem, out_sem
        self.sources = sources

    def load(self, o, h, k):
        buf, _, _, x_in, _, _ = self.refs
        return pltpu.make_async_copy(buf.at[self.sources[o](k), pl.ds(h * GROUP, GROUP)], x_in.at[o, k], self.sems[0].at[o, k])

    def save(self, o, h):
        _, _, ab, _, staged, _ = self.refs
        return pltpu.make_async_copy(staged.at[o], ab.at[o, :, pl.ds(h * GROUP, GROUP)], self.sems[1].at[o])

    def fetch(self, o, h):
        for k in range(4):
            self.load(o, h, k).start()

    def run(self, o, h):
        _, w_ref, _, x_in, staged, stage = self.refs
        hidden = staged.shape[1]
        parts = staged.shape[3] // 128
        for k in range(4):
            self.load(o, h, k).wait()
        w_t = w_ref[o]

        def one_row(ii, carry):
            zn = jnp.concatenate([x_in[o, k, ii] for k in range(4)], axis=0)
            q = lax.dot_general(w_t, zn, (((1,), (1,)), ((), ())), preferred_element_type=F32)
            val = sigmoid(q[hidden:]) * q[:hidden]
            for p in range(parts):
                stage[p, pl.ds(ii, hidden, stride=PITCH), :] = val[:, p * 128:(p + 1) * 128]
            return carry

        lax.fori_loop(0, GROUP, one_row, 0, unroll=2)
        pl.when(h > 0)(lambda: self.save(o, h - 1).wait())
        for p in range(parts):
            full = stage[p].reshape(hidden, PITCH, 128)
            staged[o, :, :, p * 128:(p + 1) * 128] = full[:, :GROUP].astype(BF16)
        self.save(o, h).start()


class Preparer:
    def __init__(self, turned, z_ref, mask_ref, ln_ref, wg_ref, buf, gate, z_in, z_turned, z_out, g_out, sems, own):
        self.turned = turned
        self.z_turned = z_turned
        self.refs = z_ref, mask_ref, ln_ref, wg_ref, buf, gate
        self.scratch = z_in, z_out, g_out
        self.sems = sems
        self.own = own

    def load(self, h, turned):
        z_ref = self.refs[0]
        rows = pl.ds(h * GROUP, GROUP)
        if turned:
            return pltpu.make_async_copy(z_ref.at[:, rows], self.z_turned.at[h % 2], self.sems.at[0, h % 2])
        return pltpu.make_async_copy(z_ref.at[rows], self.scratch[0].at[h % 2], self.sems.at[0, h % 2])

    def save_own(self, h):
        return pltpu.make_async_copy(self.scratch[1].at[h % 2], self.refs[4].at[self.own, pl.ds(h * GROUP, GROUP)], self.sems.at[1, h % 2])

    def save_gate(self, h):
        return pltpu.make_async_copy(self.scratch[2].at[h % 2], self.refs[5].at[pl.ds(h * GROUP, GROUP)], self.sems.at[2, h % 2])

    def own_chunk(self, h, chunks):
        _, mask_ref, ln_ref, _, _, _ = self.refs
        z_in, z_out, _ = self.scratch
        pl.when(h + 1 < chunks)(lambda: self.load(h + 1, self.turned).start())
        self.load(h, self.turned).wait()
        ln = ln_ref[...]
        mask = mask_ref[h]
        for ii in range(GROUP):
            if self.turned:
                z = self.z_turned[h % 2, :, ii, :]
            else:
                z = z_in[h % 2, ii]
            z_out[h % 2, ii] = (layer_norm_rows(z, ln) * mask[:, ii:ii + 1]).astype(BF16)
        self.save_own(h).start()
        self.save_own(h).wait()

    def gate_chunk(self, h, chunks):
        _, _, ln_ref, wg_ref, _, _ = self.refs
        z_in, _, g_out = self.scratch
        pl.when(h + 1 < chunks)(lambda: self.load(h + 1, False).start())
        self.load(h, False).wait()
        pl.when(h >= 2)(lambda: self.save_gate(h - 2).wait())
        ln = ln_ref[...]
        w_g = wg_ref[...]
        for ii in range(GROUP):
            zn = layer_norm_rows(z_in[h % 2, ii], ln).astype(BF16)
            g_out[h % 2, ii] = sigmoid(jnp.dot(zn, w_g, preferred_element_type=F32))
        self.save_gate(h).start()

    def end_gate(self, chunks):
        for h in range(max(0, chunks - 2), chunks):
            self.save_gate(h).wait()


def relay_out_kernel(n_z, z_ref, mask_ref, ln_ref, wg_ref, w_ref, buf, ab, gate, z_in, z_turned, z_out, g_out, prep_sem,
                     x_in, staged, stage, in_sem, out_sem, send_r, send_l, recv_z, send_p, send_q, recv_b, send_f):
    z = lax.axis_index("dap2")
    r = lax.axis_index("dap")
    chunks = buf.shape[1] // GROUP
    prep = Preparer(False, z_ref, mask_ref, ln_ref, wg_ref, buf, gate, z_in, z_turned, z_out, g_out, prep_sem, z)
    prep.load(0, False).start()
    greet(z, r, n_z)
    right, left = line_copies(buf, z, send_r, send_l, recv_z)
    b_base = jnp.where(r == z, 0, n_z)
    proj = Projector(buf, w_ref, ab, x_in, staged, stage, in_sem, out_sem, (lambda k: k, lambda k: b_base + k))

    def to_near(slot, h):
        return copy_to(buf, slot, n_z + slot, h, send_p.at[slot, h], recv_b.at[slot, h], {"dap": r ^ 1})

    def to_far(slot, h):
        return copy_to(buf, slot, n_z + slot, h, send_q.at[slot, h], recv_b.at[slot, h], {"dap": r ^ 2})

    def onward(slot, h):
        return copy_to(buf, n_z + slot, n_z + slot, h, send_f.at[slot, h], recv_b.at[slot, h], {"dap": r ^ 1})

    def spread(slot, h):
        @pl.when(r == z)
        def _():
            to_far(slot, h).start()
            to_near(slot, h).start()

    def pass_on(slot, h):
        @pl.when(r == z ^ 2)
        def _():
            onward(slot, h).wait_recv()
            onward(slot, h).start()

    def pass_on_step(t, h):
        pl.when(z - t >= 0)(lambda: pass_on(z - t, h))
        pl.when(z + t < n_z)(lambda: pass_on(z + t, h))

    def land_b(h):
        @pl.when((r == z ^ 1) | (r == z ^ 3))
        def _():
            for slot in range(n_z):
                onward(slot, h).wait_recv()

    @pl.loop(0, chunks)
    def _(h):
        prep.own_chunk(h, chunks)
        start_line(right, left, z, h, n_z)
        spread(z, h)

    prep.load(0, False).start()

    @pl.loop(0, chunks)
    def _(h):
        arrive_line(right, left, z, 1, h, n_z, spread)
        prep.gate_chunk(h, chunks)
        pass_on(z, h)
        pl.when(h >= 2)(lambda: pass_on_step(1, h - 2))

    @pl.loop(0, chunks)
    def _(h):
        arrive_line(right, left, z, 2, h, n_z, spread)
        pl.when(h >= 2)(lambda: pass_on_step(2, h - 2))
        pl.when(h < 2)(lambda: pass_on_step(1, h + chunks - 2))

    @pl.loop(0, chunks + LAG_B)
    def _(h):
        @pl.when(h < chunks)
        def _():
            arrive_line(right, left, z, 3, h, n_z, spread)
            proj.fetch(0, h)

        pl.when(h < 2)(lambda: pass_on_step(2, h + chunks - 2))
        pl.when((h >= 2) & (h < chunks + 2))(lambda: pass_on_step(3, h - 2))

        @pl.when(h >= LAG_B)
        def _():
            land_b(h - LAG_B)
            proj.fetch(1, h - LAG_B)

        pl.when(h < chunks)(lambda: proj.run(0, h))
        pl.when(h >= LAG_B)(lambda: proj.run(1, h - LAG_B))

    prep.end_gate(chunks)
    for o in range(2):
        proj.save(o, chunks - 1).wait()
    drain_line(right, left, z, n_z, chunks)
    for slot in range(n_z):
        @pl.loop(0, chunks)
        def _(h):
            @pl.when(r == z)
            def _():
                to_far(slot, h).wait_send()
                to_near(slot, h).wait_send()

            pl.when(r == z ^ 2)(lambda: onward(slot, h).wait_send())


def relay_in_kernel(n_z, z_ref, mask_ref, ln_ref, wg_ref, w_ref, buf, ab, gate, z_in, z_turned, z_out, g_out, prep_sem,
                    x_in, staged, stage, in_sem, out_sem, send_r, send_l, recv_z, send_a, recv_a, recv_b, send_p, send_q, send_f):
    z = lax.axis_index("dap2")
    r = lax.axis_index("dap")
    chunks = buf.shape[1] // GROUP
    prep = Preparer(True, z_ref, mask_ref, ln_ref, wg_ref, buf, gate, z_in, z_turned, z_out, g_out, prep_sem, z)
    prep.load(0, True).start()
    greet(z, r, n_z)
    right, left = line_copies(buf, z, send_r, send_l, recv_z)

    def b_source(k):
        return jnp.where(r == k, z, 2 * n_z + k)

    def a_source(k):
        return jnp.where(r == z, b_source(k), jnp.where(r == k, k, n_z + k))

    proj = Projector(buf, w_ref, ab, x_in, staged, stage, in_sem, out_sem, (a_source, b_source))

    def to_owner(slot, h):
        return copy_to(buf, slot, n_z + r, h, send_a.at[slot, h], recv_a.at[r, h], {"dap": slot})

    def from_peer(peer, h):
        return copy_to(buf, r, n_z + peer, h, send_a.at[peer, h], recv_a.at[peer, h], {"dap": peer})

    def to_near(h):
        return copy_to(buf, z, 2 * n_z + r, h, send_p.at[h], recv_b.at[r, h], {"dap": r ^ 1})

    def to_far(h):
        return copy_to(buf, z, 2 * n_z + r, h, send_q.at[h], recv_b.at[r, h], {"dap": r ^ 2})

    def onward(h):
        return copy_to(buf, 2 * n_z + (r ^ 2), 2 * n_z + (r ^ 2), h, send_f.at[h], recv_b.at[r ^ 2, h], {"dap": r ^ 1})

    def from_b(peer, h):
        return copy_to(buf, z, 2 * n_z + peer, h, send_p.at[h], recv_b.at[peer, h], {"dap": r ^ 1})

    def spread(slot, h):
        pl.when(slot != r)(lambda: to_owner(slot, h).start())

    @pl.loop(0, chunks)
    def _(h):
        prep.own_chunk(h, chunks)
        start_line(right, left, z, h, n_z)
        to_far(h).start()
        to_near(h).start()

    prep.load(0, False).start()

    @pl.loop(0, chunks)
    def _(h):
        arrive_line(right, left, z, 1, h, n_z, spread)
        prep.gate_chunk(h, chunks)

    @pl.loop(0, chunks)
    def _(h):
        arrive_line(right, left, z, 2, h, n_z, spread)
        onward(h).wait_recv()
        onward(h).start()

    @pl.loop(0, chunks + LAG_A)
    def _(h):
        @pl.when(h < chunks)
        def _():
            arrive_line(right, left, z, 3, h, n_z, spread)
            from_b(r ^ 1, h).wait_recv()
            from_b(r ^ 3, h).wait_recv()
            proj.fetch(1, h)

        @pl.when(h >= LAG_A)
        def _():
            @pl.when(r != z)
            def _():
                for m in (1, 2, 3):
                    from_peer(r ^ m, h - LAG_A).wait_recv()

            proj.fetch(0, h - LAG_A)

        pl.when(h < chunks)(lambda: proj.run(1, h))
        pl.when(h >= LAG_A)(lambda: proj.run(0, h - LAG_A))

    prep.end_gate(chunks)
    for o in range(2):
        proj.save(o, chunks - 1).wait()
    drain_line(right, left, z, n_z, chunks)

    @pl.loop(0, chunks)
    def _(h):
        to_far(h).wait_send()
        to_near(h).wait_send()
        onward(h).wait_send()
        for slot in range(n_z):
            pl.when((slot != z) & (slot != r))(lambda: to_owner(slot, h).wait_send())


def relay(kernel, n_slots, state, mask_g, ln, w_g, w_abt, sems, collective_id, name):
    rows, cols, width = state.shape
    hidden = w_abt.shape[1] // 2
    depth = 4 * cols
    in_hbm = pl.BlockSpec(memory_space=pl.ANY)
    in_vmem = pl.BlockSpec(memory_space=pltpu.VMEM)
    return pl.pallas_call(
        kernel,
        out_shape=[
            jax.ShapeDtypeStruct((n_slots, rows, cols, width), BF16),
            jax.ShapeDtypeStruct((2, hidden, rows, depth), BF16),
            jax.ShapeDtypeStruct(state.shape, F32),
        ],
        in_specs=[in_hbm, in_vmem, in_vmem, in_vmem, in_vmem],
        out_specs=[in_hbm, in_hbm, in_hbm],
        scratch_shapes=[
            pltpu.VMEM((2, GROUP, cols, width), F32),
            pltpu.VMEM((2, rows, GROUP, width), F32),
            pltpu.VMEM((2, GROUP, cols, width), BF16),
            pltpu.VMEM((2, GROUP, cols, width), F32),
            pltpu.SemaphoreType.DMA((3, 2)),
            pltpu.VMEM((2, 4, GROUP, cols, width), BF16),
            pltpu.VMEM((2, hidden, GROUP, depth), BF16),
            pltpu.VMEM((depth // 128, hidden * PITCH, 128), F32),
            pltpu.SemaphoreType.DMA((2, 4)),
            pltpu.SemaphoreType.DMA((2,)),
        ] + [pltpu.SemaphoreType.DMA(s) for s in sems],
        compiler_params=pltpu.CompilerParams(
            collective_id=collective_id, has_side_effects=True, vmem_limit_bytes=48 * 1024 * 1024
        ),
        name=name,
    )(state, mask_g, ln, w_g, w_abt)[1:]


def finish_kernel(n_mul, a_ref, b_ref, z_ref, gate_ref, lnx_ref, wo_ref, out_ref, x_lo, x_hi):
    rows = a_ref.shape[2]
    cols = z_ref.shape[1]
    hidden = wo_ref.shape[0]
    lo = min(cols, 128)
    s = pl.program_id(0)

    @pl.when(s < n_mul)
    def _():
        for cc in range(CHAN_BLOCK):
            x = lax.dot_general(a_ref[0, cc], b_ref[0, cc], (((1,), (1,)), ((), ())), preferred_element_type=F32)
            at = pl.multiple_of((s * CHAN_BLOCK + cc) * (rows + PAD), 8)
            x_lo[pl.ds(at, rows), :lo] = x[:, :lo]
            if cols > lo:
                x_hi[pl.ds(at, rows), :cols - lo] = x[:, lo:]

    @pl.when(s >= n_mul)
    def _():
        first = (s - n_mul) * GROUP
        w_o = wo_ref[...]
        gain = lnx_ref[:, 0:1]
        bias = lnx_ref[:, 1:2]

        def normed(x):
            mean = jnp.mean(x, axis=0, keepdims=True)
            centered = x - mean
            variance = jnp.mean(centered * centered, axis=0, keepdims=True)
            return (centered * lax.rsqrt(variance + LN_EPS) * gain + bias).astype(BF16)

        for ii in range(GROUP):
            row = pl.ds(first + ii, hidden, stride=rows + PAD)
            xn = normed(x_lo[row, :][:, :lo])
            if cols > lo:
                xn = jnp.concatenate([xn, normed(x_hi[row, :][:, :cols - lo])], axis=1)
            y = lax.dot_general(xn, w_o, (((0,), (0,)), ((), ())), preferred_element_type=F32)
            out_ref[ii] = z_ref[ii] + gate_ref[ii] * y


def finish(ab, z, gate, ln_x, w_o):
    rows, cols, width = z.shape
    hidden, depth = ab.shape[1], ab.shape[3]
    n_mul = hidden // CHAN_BLOCK

    def tile(i):
        return (jnp.maximum(i - n_mul, 0), 0, 0)

    def whole(i):
        return (0, 0)

    return pl.pallas_call(
        functools.partial(finish_kernel, n_mul),
        out_shape=jax.ShapeDtypeStruct(z.shape, F32),
        grid=(n_mul + rows // GROUP,),
        in_specs=[
            pl.BlockSpec((1, CHAN_BLOCK, rows, depth), lambda i: (0, jnp.minimum(i, n_mul - 1), 0, 0)),
            pl.BlockSpec((1, CHAN_BLOCK, rows, depth), lambda i: (1, jnp.minimum(i, n_mul - 1), 0, 0)),
            pl.BlockSpec((GROUP, cols, width), tile),
            pl.BlockSpec((GROUP, cols, width), tile),
            pl.BlockSpec((hidden, 2), whole),
            pl.BlockSpec((hidden, width), whole),
        ],
        out_specs=pl.BlockSpec((GROUP, cols, width), tile),
        scratch_shapes=[pltpu.VMEM((hidden * (rows + PAD), 128), F32)] * 2,
        compiler_params=pltpu.CompilerParams(vmem_limit_bytes=62 * 1024 * 1024),
        name="finish",
    )(ab, ab, z, gate, ln_x, w_o)


def solution(mesh):
    n_z = mesh.shape["dap2"]
    pair_spec = P(("data", "dap"), "dap2", None)
    mask_spec = P(("data", "dap"), "dap2")

    def local_stack(pair_act, pair_mask, ln_z, w_ab, w_g, ln_x, w_o):
        rows, cols, _ = pair_act.shape
        chunks = rows // GROUP
        sems = [[(n_z, chunks)] * 7, [(n_z, chunks)] * 6 + [(chunks,)] * 3]
        mask = pair_mask.astype(F32)
        masks = [m.reshape(cols, chunks, GROUP).transpose(1, 0, 2) for m in (mask.T, mask)]
        kernels = [relay_out_kernel, relay_in_kernel]
        state = pair_act
        for layer in range(w_o.shape[0]):
            for upd in range(2):
                ab, gate = relay(
                    functools.partial(kernels[upd], n_z),
                    (2 + upd) * n_z,
                    state,
                    masks[upd],
                    ln_z[layer, upd].astype(F32),
                    w_g[layer, upd],
                    w_ab[layer, upd].T.reshape(2, -1, w_ab.shape[2]),
                    sems[upd],
                    2 * layer + upd,
                    f"relay_{layer}_{upd}",
                )
                state = finish(ab, state, gate, ln_x[layer, upd].astype(F32).T, w_o[layer, upd])
        return state

    return jax.shard_map(local_stack, mesh=mesh, in_specs=(pair_spec, mask_spec, P(), P(), P(), P(), P()), out_specs=pair_spec, check_vma=False)
```

time: 2410 us -> 1000 us (0.41)
  blocking collectives: 1380 us -> 0 us
  Pallas kernels: 0 us -> 995 us
  waiting for transfers between devices: 503 us -> 0 us
  local copies, waits for them, and re-layouts: 215 us -> 3.59 us
  matrix products: 172 us -> 0 us
  other arithmetic: 115 us -> 2.91 us
    all_to_all x8 -> x0, blocking collectives: 1380 us -> none  [the longest x2 474 us: to_transposed(): stage_one = lax.all_to_all(blocks, 'dap2', 1, 2, tiled=True)]
    pallas_call x0 -> x4, Pallas kernels: none -> 995 us  [the longest x2 917 us: relay(): pl.pallas_call(kernel, out_shape=[jax.ShapeDtypeStruct((n_slots, rows, co...]
    all_gather x4 -> x0, waiting for transfers between devices: 502 us -> none  [the longest x1 381 us: tri_update(): lax.all_gather(to_transposed(a_proj, row_devs, col_devs), 'dap2', axis=1,...]
    dot_general x8 -> x0, matrix products: 172 us -> none  [the longest x2 51.6 us: finish_local(): jnp.einsum('cij,cd->ijd', x_norm, w_o, preferred_element_type=jnp.float32)]
    all_gather x4 -> x0, local copies, waits for them, and re-layouts: 166 us -> none  [the longest x1 56.7 us: tri_update(): b_cols = lax.all_gather(b_proj, 'dap', axis=1, tiled=True)]
    convert_element_type x7 -> x2, other arithmetic: 61.7 us -> 1.63 us  [the longest x1 0.96 us: local_stack(): mask = pair_mask.astype(F32)]
    reduce_sum x5 -> x0, other arithmetic: 53.3 us -> none  [the longest x2 23.8 us: norm_last(): variance = jnp.mean(centered * centered, axis=-1, keepdims=True)]
    all_to_all x11 -> x0, local copies, waits for them, and re-layouts: 41.4 us -> none  [the longest x2 21.3 us: to_transposed(): stage_one = lax.all_to_all(blocks, 'dap2', 1, 2, tiled=True)]
  transfers between devices with their start and end apart: 4 -> 0, of which waited for: 2 -> 0; matrix products, arithmetic and copies ran while one was open for 7% -> 0% of each run, Pallas kernels for 0% -> 0%
where the time goes in v2:
time: 1000 us
  Pallas kernels  995 us (100%)
    pallas_call x2, Pallas kernels, relay(): pl.pallas_call(kernel, out_shape=[jax.ShapeDtypeStruct((n_slots, rows, co...  917 us
    pallas_call x2, Pallas kernels, finish(): pl.pallas_call(functools.partial(finish_kernel, n_mul), out_shape=jax.Sha...  78.1 us

profile of v2, /device:TPU:0, one launch (start us, length us, event | category | flops | bytes accessed | tf_op | source)
XLA Modules:
  0.0 1001.2 jit_solution(14190351588283637175)
XLA Ops:
  0.0 0.0 copy-start.1
  0.0 0.0 copy-start
  0.0 1.0 convert_element_type.21
  1.0 0.3 copy.12
  1.3 1.0 slice_bitcast_fusion
  2.2 0.1 copy.13
  2.4 0.8 slice_bitcast_fusion.3
  3.2 0.7 bitcast_convert_fusion
  3.8 463.1 %relay_0_0.1 = (bf16[8,160,160,128]{3,2,1,0:T(8,128)(2,1)}, bf16[2,128,160,640]{3,2,1,0:T(8,128)(2,1)}, f32[160,160,128]{2,1,0:T(8,128)}) custom-call(f32[160,160,128]{2,1,0:T(8,128)} %z_ref.3, f32[10,160,16]{2,1,0:T(8,128)S(1)} %bitcast.40, f32[2,128]{1,0:T(2,128)S(1)} %get-tuple-element.22.ln_ref, bf16[128,128]{1,0:T(8,128)(2,1)S(1)} %get-tuple-element.18.wg_ref, ...), custom_call_target="tpu_custom_call" | custom-call | tf_op jit(solution)/shard_map/relay_0_0/pallas_call | solution.py:392
  467.0 0.0 copy-done.1
  467.0 0.1 copy.14
  467.1 0.6 convert_bitcast_fusion.1.lnx_ref
  467.8 0.0 copy-done
  467.8 0.6 slice_bitcast_fusion.2
  468.4 39.1 %finish.2.z_ref = f32[160,160,128]{2,1,0:T(8,128)} custom-call(bf16[2,128,160,640]{3,2,1,0:T(8,128)(2,1)} %get-tuple-element.9.a_ref.b_ref, bf16[2,128,160,640]{3,2,1,0:T(8,128)(2,1)} %get-tuple-element.9.a_ref.b_ref, f32[160,160,128]{2,1,0:T(8,128)} %z_ref.3, f32[160,160,128]{2,1,0:T(8,128)} %get-tuple-element.10.gate_ref, ...), custom_call_target="tpu_custom_call" | custom-call | tf_op jit(solution)/shard_map/finish/pallas_call | solution.py:469
  507.4 0.1 copy.15
  507.6 0.3 copy.16
  507.8 0.1 copy.17
  508.0 453.4 %relay_0_1.1 = (bf16[12,160,160,128]{3,2,1,0:T(8,128)(2,1)}, bf16[2,128,160,640]{3,2,1,0:T(8,128)(2,1)}, f32[160,160,128]{2,1,0:T(8,128)}) custom-call(f32[160,160,128]{2,1,0:T(8,128)} %finish.2.z_ref, f32[10,160,16]{2,1,0:T(8,128)S(1)} %bitcast.41, f32[2,128]{1,0:T(2,128)S(1)} %get-tuple-element.21.ln_ref, bf16[128,128]{1,0:T(8,128)(2,1)S(1)} %get-tuple-element.17.wg_ref, ...), custom_call_target="tpu_custom_call" | custom-call | tf_op jit(solution)/shard_map/relay_0_1/pallas_call | solution.py:392
  961.4 0.1 copy.18
  961.5 0.6 convert_bitcast_fusion.lnx_ref
  962.1 39.0 %finish.3 = f32[160,160,128]{2,1,0:T(8,128)} custom-call(bf16[2,128,160,640]{3,2,1,0:T(8,128)(2,1)} %get-tuple-element.11.a_ref.b_ref, bf16[2,128,160,640]{3,2,1,0:T(8,128)(2,1)} %get-tuple-element.11.a_ref.b_ref, f32[160,160,128]{2,1,0:T(8,128)} %finish.2.z_ref, f32[160,160,128]{2,1,0:T(8,128)} %get-tuple-element.12.gate_ref, ...), custom_call_target="tpu_custom_call" | custom-call | tf_op jit(solution)/shard_map/finish/pallas_call | solution.py:469
  (1 shorter events, 0.0 us)
Async XLA Ops:
  0.0 467.0 %copy-start.1 = (bf16[1,2,2,128]{3,2,1,0:T(2,128)(2,1)S(1)}, bf16[1,2,2,128]{3,2,1,0:T(2,128)(2,1)}, u32[]{:S(2)}) copy-start(bf16[1,2,2,128]{3,2,1,0:T(2,128)(2,1)} %param.12) | copy-start | bytes 3076
  0.0 467.8 %copy-start = (bf16[1,2,128,128]{3,2,1,0:T(8,128)(2,1)S(1)}, bf16[1,2,128,128]{3,2,1,0:T(8,128)(2,1)}, u32[]{:S(2)}) copy-start(bf16[1,2,128,128]{3,2,1,0:T(8,128)(2,1)} %param.13) | copy-start | bytes 196612

commit v3 on v2

--- a/solution.py
+++ b/solution.py
@@ -11,8 +11,8 @@
 GROUP = 16
 CHAN_BLOCK = 16
 PITCH = 24
-PAD = 8
-LAG_B = 3
+PAD = 4
+LAG_B = 1
 LAG_A = 2
 F32 = jnp.float32
 BF16 = jnp.bfloat16
@@ -40,6 +40,10 @@
         hello({"dap": r ^ m})
     pl.when(z > 0)(lambda: hello({"dap2": z - 1}))
     pl.when(z < n_z - 1)(lambda: hello({"dap2": z + 1}))
+
+
+def meet(z, n_z):
+    barrier = pltpu.get_barrier_semaphore()
     inner = (z > 0) & (z < n_z - 1)
     pl.when(inner)(lambda: pl.semaphore_wait(barrier, 5))
     pl.when(jnp.logical_not(inner))(lambda: pl.semaphore_wait(barrier, 4))
@@ -128,7 +132,7 @@
                 stage[p, pl.ds(ii, hidden, stride=PITCH), :] = val[:, p * 128:(p + 1) * 128]
             return carry
 
-        lax.fori_loop(0, GROUP, one_row, 0, unroll=2)
+        lax.fori_loop(0, GROUP, one_row, 0, unroll=8)
         pl.when(h > 0)(lambda: self.save(o, h - 1).wait())
         for p in range(parts):
             full = stage[p].reshape(hidden, PITCH, 128)
@@ -238,6 +242,7 @@
     @pl.loop(0, chunks)
     def _(h):
         prep.own_chunk(h, chunks)
+        pl.when(h == 0)(lambda: meet(z, n_z))
         start_line(right, left, z, h, n_z)
         spread(z, h)
 
@@ -248,13 +253,13 @@
         arrive_line(right, left, z, 1, h, n_z, spread)
         prep.gate_chunk(h, chunks)
         pass_on(z, h)
-        pl.when(h >= 2)(lambda: pass_on_step(1, h - 2))
+        pl.when(h >= 1)(lambda: pass_on_step(1, h - 1))
 
     @pl.loop(0, chunks)
     def _(h):
         arrive_line(right, left, z, 2, h, n_z, spread)
-        pl.when(h >= 2)(lambda: pass_on_step(2, h - 2))
-        pl.when(h < 2)(lambda: pass_on_step(1, h + chunks - 2))
+        pl.when(h >= 1)(lambda: pass_on_step(2, h - 1))
+        pl.when(h < 1)(lambda: pass_on_step(1, chunks - 1))
 
     @pl.loop(0, chunks + LAG_B)
     def _(h):
@@ -263,8 +268,8 @@
             arrive_line(right, left, z, 3, h, n_z, spread)
             proj.fetch(0, h)
 
-        pl.when(h < 2)(lambda: pass_on_step(2, h + chunks - 2))
-        pl.when((h >= 2) & (h < chunks + 2))(lambda: pass_on_step(3, h - 2))
+        pl.when(h < 1)(lambda: pass_on_step(2, chunks - 1))
+        pl.when(h >= 1)(lambda: pass_on_step(3, h - 1))
 
         @pl.when(h >= LAG_B)
         def _():
@@ -331,6 +336,7 @@
     @pl.loop(0, chunks)
     def _(h):
         prep.own_chunk(h, chunks)
+        pl.when(h == 0)(lambda: meet(z, n_z))
         start_line(right, left, z, h, n_z)
         to_far(h).start()
         to_near(h).start()
@@ -428,7 +434,7 @@
     def _():
         for cc in range(CHAN_BLOCK):
             x = lax.dot_general(a_ref[0, cc], b_ref[0, cc], (((1,), (1,)), ((), ())), preferred_element_type=F32)
-            at = pl.multiple_of((s * CHAN_BLOCK + cc) * (rows + PAD), 8)
+            at = pl.multiple_of(s * (CHAN_BLOCK * (rows + PAD)), 8) + cc * (rows + PAD)
             x_lo[pl.ds(at, rows), :lo] = x[:, :lo]
             if cols > lo:
                 x_hi[pl.ds(at, rows), :cols - lo] = x[:, lo:]

time: 1000 us -> 978 us (0.978)
  Pallas kernels: 995 us -> 969 us
    pallas_call x2, Pallas kernels: 917 us -> 893 us  [relay(): pl.pallas_call(kernel, out_shape=[jax.ShapeDtypeStruct((n_slots, rows, co...]
where the time goes in v3:
time: 978 us; the launch traced here: 976 us
  Pallas kernels  969 us (99%)
    pallas_call x2, Pallas kernels, relay(): pl.pallas_call(kernel, out_shape=[jax.ShapeDtypeStruct((n_slots, rows, co...  893 us
    pallas_call x2, Pallas kernels, finish(): pl.pallas_call(functools.partial(finish_kernel, n_mul), out_shape=jax.Sha...  76.4 us

profile of v3, /device:TPU:0, one launch (start us, length us, event | category | flops | bytes accessed | tf_op | source)
XLA Modules:
  0.0 976.0 jit_solution(6031208372973716042)
XLA Ops:
  0.0 0.0 copy-start.1
  0.0 0.0 copy-start
  0.0 1.0 convert_element_type.21
  1.0 0.3 copy.12
  1.3 1.0 slice_bitcast_fusion
  2.2 0.1 copy.13
  2.4 0.8 slice_bitcast_fusion.3
  3.2 0.7 bitcast_convert_fusion
  3.8 447.2 %relay_0_0.1 = (bf16[8,160,160,128]{3,2,1,0:T(8,128)(2,1)}, bf16[2,128,160,640]{3,2,1,0:T(8,128)(2,1)}, f32[160,160,128]{2,1,0:T(8,128)}) custom-call(f32[160,160,128]{2,1,0:T(8,128)} %z_ref.3, f32[10,160,16]{2,1,0:T(8,128)S(1)} %bitcast.40, f32[2,128]{1,0:T(2,128)S(1)} %get-tuple-element.22.ln_ref, bf16[128,128]{1,0:T(8,128)(2,1)S(1)} %get-tuple-element.18.wg_ref, ...), custom_call_target="tpu_custom_call" | custom-call | tf_op jit(solution)/shard_map/relay_0_0/pallas_call | solution.py:398
  451.0 0.0 copy-done.1
  451.1 0.1 copy.14
  451.2 0.6 convert_bitcast_fusion.1.lnx_ref
  451.8 0.0 copy-done
  451.8 0.6 slice_bitcast_fusion.2
  452.5 38.2 %finish.2.z_ref = f32[160,160,128]{2,1,0:T(8,128)} custom-call(bf16[2,128,160,640]{3,2,1,0:T(8,128)(2,1)} %get-tuple-element.9.a_ref.b_ref, bf16[2,128,160,640]{3,2,1,0:T(8,128)(2,1)} %get-tuple-element.9.a_ref.b_ref, f32[160,160,128]{2,1,0:T(8,128)} %z_ref.3, f32[160,160,128]{2,1,0:T(8,128)} %get-tuple-element.10.gate_ref, ...), custom_call_target="tpu_custom_call" | custom-call | tf_op jit(solution)/shard_map/finish/pallas_call | solution.py:475
  490.7 0.1 copy.15
  490.8 0.3 copy.16
  491.1 0.1 copy.17
  491.2 445.8 %relay_0_1.1 = (bf16[12,160,160,128]{3,2,1,0:T(8,128)(2,1)}, bf16[2,128,160,640]{3,2,1,0:T(8,128)(2,1)}, f32[160,160,128]{2,1,0:T(8,128)}) custom-call(f32[160,160,128]{2,1,0:T(8,128)} %finish.2.z_ref, f32[10,160,16]{2,1,0:T(8,128)S(1)} %bitcast.41, f32[2,128]{1,0:T(2,128)S(1)} %get-tuple-element.21.ln_ref, bf16[128,128]{1,0:T(8,128)(2,1)S(1)} %get-tuple-element.17.wg_ref, ...), custom_call_target="tpu_custom_call" | custom-call | tf_op jit(solution)/shard_map/relay_0_1/pallas_call | solution.py:398
  937.0 0.1 copy.18
  937.1 0.6 convert_bitcast_fusion.lnx_ref
  937.8 38.2 %finish.3 = f32[160,160,128]{2,1,0:T(8,128)} custom-call(bf16[2,128,160,640]{3,2,1,0:T(8,128)(2,1)} %get-tuple-element.11.a_ref.b_ref, bf16[2,128,160,640]{3,2,1,0:T(8,128)(2,1)} %get-tuple-element.11.a_ref.b_ref, f32[160,160,128]{2,1,0:T(8,128)} %finish.2.z_ref, f32[160,160,128]{2,1,0:T(8,128)} %get-tuple-element.12.gate_ref, ...), custom_call_target="tpu_custom_call" | custom-call | tf_op jit(solution)/shard_map/finish/pallas_call | solution.py:475
  (1 shorter events, 0.0 us)
Async XLA Ops:
  0.0 451.0 %copy-start.1 = (bf16[1,2,2,128]{3,2,1,0:T(2,128)(2,1)S(1)}, bf16[1,2,2,128]{3,2,1,0:T(2,128)(2,1)}, u32[]{:S(2)}) copy-start(bf16[1,2,2,128]{3,2,1,0:T(2,128)(2,1)} %param.12) | copy-start | bytes 3076
  0.0 451.8 %copy-start = (bf16[1,2,128,128]{3,2,1,0:T(8,128)(2,1)S(1)}, bf16[1,2,128,128]{3,2,1,0:T(8,128)(2,1)}, u32[]{:S(2)}) copy-start(bf16[1,2,128,128]{3,2,1,0:T(8,128)(2,1)} %param.13) | copy-start | bytes 196612
